TPU v7x, 128 devices: a whole 4x4x4 slice. The times are simulated.
128 devices in a mesh: fsdp: 16 (over z, x), tp: 8 (over y, core).
Axes of the slice: x: 4, y: 4, z: 4, core: 2. Of those that a mesh axis runs over, the one named last changes fastest.
Arguments:
- weight_query: bfloat16 [12288, 12288], P('fsdp', 'tp'), may hold values from -0.078125 to 0.078125
- low_query: bfloat16 [12288, 64], P('fsdp'), may hold values from -0.0546875 to 0.0546875
- high_query: bfloat16 [64, 12288], P(None, 'tp'), may hold values from -0.75 to 0.75
- weight_key: bfloat16 [12288, 12288], P('fsdp', 'tp'), may hold values from -0.078125 to 0.078125
- low_key: bfloat16 [12288, 64], P('fsdp'), may hold values from -0.0546875 to 0.0546875
- high_key: bfloat16 [64, 12288], P(None, 'tp'), may hold values from -0.75 to 0.75
- weight_value: bfloat16 [12288, 12288], P('fsdp', 'tp'), may hold values from -0.078125 to 0.078125
- low_value: bfloat16 [12288, 64], P('fsdp'), may hold values from -0.0546875 to 0.0546875
- high_value: bfloat16 [64, 12288], P(None, 'tp'), may hold values from -0.75 to 0.75
- norm_train: float32 [12288], P(('fsdp', 'tp')), may hold values from 0.25 to 1.75
- norm_step: float32 [12288], P(('fsdp', 'tp')), may hold values from -0.3 to 0.3
Outputs:
- ready_query: bfloat16 [12288, 12288], P(None, ('tp', 'fsdp'))
- ready_key: bfloat16 [12288, 12288], P(None, ('tp', 'fsdp'))
- ready_value: bfloat16 [12288, 12288], P(None, ('tp', 'fsdp'))
- factor_query: float32 [12288], P(('tp', 'fsdp'))
- factor_key: float32 [12288], P(('tp', 'fsdp'))
- factor_value: float32 [12288], P(('tp', 'fsdp'))
- serve_norm: bfloat16 [12288], replicated
All inputs are finite; a program needn't handle non-finite values. Where the computation divides by a largest or mean magnitude, that divisor is 1e-20 or more.
Results may differ from a plain program's by a relative error of at most 0.001.
Values may be sent and summed in bfloat16 or wider, within the bound.
A program may use at most 128 MiB of HBM per device.

v0:
```python
import jax
import jax.numpy as jnp
from jax import lax
from jax.sharding import Mesh
from jax.sharding import PartitionSpec as P

FSDP = ("fsdp_0", "fsdp_1")
FSDP_TP = ("fsdp_0", "fsdp_1", "tp_0", "tp_1")
TP = ("tp_0", "tp_1")
TP_FSDP = ("tp_0", "tp_1", "fsdp_0", "fsdp_1")


mix_rate = 2.0


def copy_for_each(x, axis):
    copies = jnp.broadcast_to(x, (lax.axis_size(axis), *x.shape))
    return lax.all_to_all(copies, axis, split_axis=0, concat_axis=0, tiled=True)


def of_everyone(x, axis):
    everything = copy_for_each(x, axis)
    return jnp.max(everything, axis=0)


def packed_total(arrays, axis):
    ends = [0]
    for a in arrays:
        ends.append(ends[-1] + a.size)
    total = of_everyone(jnp.concatenate([a.ravel() for a in arrays]), axis)
    return tuple((total[b:e].reshape(a.shape) for a, b, e in zip(arrays, ends, ends[1:])))


def joined_along(parts, dim):
    lengths = list(parts.shape[1:])
    lengths[dim] *= parts.shape[0]
    return jnp.moveaxis(parts, 0, dim).reshape(lengths)


def whole_of(x, axes, dim):
    far, near = axes
    leading = copy_for_each(x, far)
    parts = jnp.swapaxes(copy_for_each(leading, near), 0, 1)
    return joined_along(parts.reshape(-1, *x.shape), dim)


def local(
    weight_query,
    low_query,
    high_query,
    weight_key,
    low_key,
    high_key,
    weight_value,
    low_value,
    high_value,
    norm_train,
    norm_step,
):
    latest_query = weight_query.astype(jnp.float32) + mix_rate * jnp.dot(
        low_query, high_query, preferred_element_type=jnp.float32
    )
    latest_key = weight_key.astype(jnp.float32) + mix_rate * jnp.dot(
        low_key, high_key, preferred_element_type=jnp.float32
    )
    latest_value = weight_value.astype(jnp.float32) + mix_rate * jnp.dot(
        low_value, high_value, preferred_element_type=jnp.float32
    )
    factor_query, factor_key, factor_value = packed_total(
        (
            jnp.max(jnp.abs(latest_query), axis=0),
            jnp.max(jnp.abs(latest_key), axis=0),
            jnp.max(jnp.abs(latest_value), axis=0),
        ),
        FSDP,
    )
    narrow_query, narrow_key, narrow_value = (
        (latest_query / factor_query).astype(jnp.bfloat16),
        (latest_key / factor_key).astype(jnp.bfloat16),
        (latest_value / factor_value).astype(jnp.bfloat16),
    )
    ready_query, ready_key, ready_value = (
        lax.all_to_all(narrow_query, FSDP, split_axis=1, concat_axis=0, tiled=True),
        lax.all_to_all(narrow_key, FSDP, split_axis=1, concat_axis=0, tiled=True),
        lax.all_to_all(narrow_value, FSDP, split_axis=1, concat_axis=0, tiled=True),
    )
    place = lax.axis_index(FSDP)
    factor_query = lax.dynamic_slice_in_dim(
        factor_query, place * ready_query.shape[1], ready_query.shape[1]
    )
    factor_key = lax.dynamic_slice_in_dim(
        factor_key, place * ready_key.shape[1], ready_key.shape[1]
    )
    factor_value = lax.dynamic_slice_in_dim(
        factor_value, place * ready_value.shape[1], ready_value.shape[1]
    )
    serve_norm = whole_of(
        (norm_train + norm_step).astype(jnp.bfloat16), (("fsdp_0", "fsdp_1", "tp_0"), "tp_1"), 0
    )
    return (ready_query, ready_key, ready_value, factor_query, factor_key, factor_value, serve_norm)


def solution(mesh):
    finer = Mesh(mesh.devices.reshape(4, 4, 4, 2), ("fsdp_0", "fsdp_1", "tp_0", "tp_1"))
    return jax.shard_map(
        local,
        mesh=finer,
        in_specs=(
            P(FSDP, TP),
            P(FSDP, None),
            P(None, TP),
            P(FSDP, TP),
            P(FSDP, None),
            P(None, TP),
            P(FSDP, TP),
            P(FSDP, None),
            P(None, TP),
            P(FSDP_TP),
            P(FSDP_TP),
        ),
        out_specs=(
            P(None, TP_FSDP),
            P(None, TP_FSDP),
            P(None, TP_FSDP),
            P(TP_FSDP),
            P(TP_FSDP),
            P(TP_FSDP),
            P(),
        ),
        check_vma=False,
    )
```

profile of v0, /device:TPU:0, one launch (start us, length us, event | category | flops | bytes accessed | tf_op | source)
XLA Modules:
  0.0 174.9 jit_solution(3834576946451534320)
XLA Ops:
  0.7 0.8 add_convert_fusion
  2.1 11.5 %all-to-all-start.4 = ((bf16[64,1,96]{2,1,0:T(2,128)(2,1)}), bf16[64,1,96]{2,1,0:T(2,128)(2,1)S(1)}, u32[]{:S(2)}, u32[]{:S(2)}) async-start(bf16[64,1,96]{2,1,0:T(2,128)(2,1)} %broadcast_in_dim.13), calls=%async_computation.4 | async-start | bytes 65536 | tf_op jit(solution)/shard_map/all_to_all | solution.py:18
  13.7 4.7 %abs_reduce_fusion.2 = (f32[1536]{0:T(1024)S(1)}, f32[768,1536]{1,0:T(8,128)}) fusion(bf16[768,64]{0,1:T(8,128)(2,1)} %param.12, bf16[64,1536]{1,0:T(8,128)(2,1)S(1)} %copy-done, bf16[768,1536]{1,0:T(8,128)(2,1)} %param.11), kind=kOutput, calls=%fused_computation.7 | convolution fusion | flops 156891648 | bytes 7378944 | tf_op jit(solution)/shard_map/dot_general | solution.py:60
  18.4 3.0 %abs_reduce_fusion = (f32[1536]{0:T(1024)S(1)}, f32[768,1536]{1,0:T(8,128)}) fusion(bf16[768,64]{0,1:T(8,128)(2,1)S(1)} %copy-done.5, bf16[64,1536]{1,0:T(8,128)(2,1)S(1)} %copy-done.3, bf16[768,1536]{1,0:T(8,128)(2,1)S(1)} %copy-done.1), kind=kOutput, calls=%fused_computation.3 | convolution fusion | flops 156891648 | bytes 7378944 | tf_op jit(solution)/shard_map/dot_general | solution.py:66
  21.4 3.0 %abs_reduce_fusion.1 = (f32[1536]{0:T(1024)S(1)}, f32[768,1536]{1,0:T(8,128)}) fusion(bf16[768,64]{0,1:T(8,128)(2,1)S(1)} %copy-done.6, bf16[64,1536]{1,0:T(8,128)(2,1)S(1)} %copy-done.4, bf16[768,1536]{1,0:T(8,128)(2,1)S(1)} %copy-done.2), kind=kOutput, calls=%fused_computation.5 | convolution fusion | flops 156891648 | bytes 7378944 | tf_op jit(solution)/shard_map/dot_general | solution.py:63
  24.4 0.9 broadcast_in_dim.12
  25.3 7.0 %all-to-all-start = ((f32[16,1,4608]{2,1,0:T(1,128)}), f32[16,1,4608]{2,1,0:T(1,128)S(1)}, u32[]{:S(2)}, u32[]{:S(2)}) async-start(f32[16,1,4608]{2,1,0:T(1,128)} %broadcast_in_dim.12), calls=%async_computation | async-start | bytes 589824 | tf_op jit(solution)/shard_map/all_to_all | solution.py:18
  32.3 8.9 %all-to-all-done = f32[16,1,4608]{2,1,0:T(1,128)S(1)} async-done(((f32[16,1,4608]{2,1,0:T(1,128)}), f32[16,1,4608]{2,1,0:T(1,128)S(1)}, u32[]{:S(2)}, u32[]{:S(2)}) %all-to-all-start) | async-done | bytes 294944 | tf_op jit(solution)/shard_map/all_to_all | solution.py:18
  41.8 3.3 %all-to-all-start.5 = ((bf16[2,64,96]{2,1,0:T(8,128)(2,1)}), bf16[2,64,96]{2,1,0:T(8,128)(2,1)S(1)}, u32[]{:S(2)}, u32[]{:S(2)}) async-start(bf16[2,64,96]{2,1,0:T(8,128)(2,1)} %broadcast_in_dim.14), calls=%async_computation.5 | async-start | bytes 65536 | tf_op jit(solution)/shard_map/all_to_all | solution.py:18
  45.3 2.9 %divide_convert_fusion.2 = bf16[768,1536]{1,0:T(8,128)(2,1)S(1)} fusion(f32[768,1536]{1,0:T(8,128)} %get-tuple-element.15, f32[1536]{0:T(1024)S(1)} %get-tuple-element.9), kind=kLoop, calls=%fused_computation.2 | loop fusion | flops 2359296 | bytes 7084032 | tf_op jit(solution)/shard_map/convert_element_type | solution.py:78
  48.2 2.4 %copy.45 = bf16[768,1536]{0,1:T(8,128)(2,1)} copy(bf16[768,1536]{1,0:T(8,128)(2,1)S(1)} %divide_convert_fusion.2) | data formatting | bytes 4718592 | tf_op jit(solution)/shard_map/convert_element_type | solution.py:78
  50.6 3.7 %all-to-all-start.1 = ((bf16[768,16,96]{0,2,1:T(8,128)(2,1)}), bf16[768,16,96]{0,2,1:T(8,128)(2,1)S(1)}, u32[]{:S(2)}, u32[]{:S(2)}) async-start(bf16[768,16,96]{0,2,1:T(8,128)(2,1)} %bitcast.24), calls=%async_computation.1 | async-start | bytes 4718592 | tf_op jit(solution)/shard_map/all_to_all | solution.py:83
  54.3 7.2 %divide_convert_fusion = (bf16[768,1536]{1,0:T(8,128)(2,1)}, bf16[768,1536]{1,0:T(8,128)(2,1)}) fusion(f32[768,1536]{1,0:T(8,128)} %get-tuple-element.11, f32[1536]{0:T(1024)S(1)} %get-tuple-element.7, f32[768,1536]{1,0:T(8,128)} %get-tuple-element.13, f32[1536]{0:T(1024)S(1)} %get-tuple-element.8), kind=kLoop, calls=%fused_computation | loop fusion | flops 4718592 | bytes 14168064 | tf_op jit(solution)/shard_map/convert_element_type | solution.py:80
  61.5 4.3 %copy.47 = bf16[768,1536]{0,1:T(8,128)(2,1)} copy(bf16[768,1536]{1,0:T(8,128)(2,1)} %get-tuple-element.17) | data formatting | bytes 4718592 | tf_op jit(solution)/shard_map/convert_element_type | solution.py:79
  65.8 27.0 %all-to-all-done.1 = bf16[768,16,96]{0,2,1:T(8,128)(2,1)S(1)} async-done(((bf16[768,16,96]{0,2,1:T(8,128)(2,1)}), bf16[768,16,96]{0,2,1:T(8,128)(2,1)S(1)}, u32[]{:S(2)}, u32[]{:S(2)}) %all-to-all-start.1) | async-done | bytes 2359328 | tf_op jit(solution)/shard_map/all_to_all | solution.py:83
  92.8 4.4 %all-to-all-start.2 = ((bf16[768,16,96]{0,2,1:T(8,128)(2,1)}), bf16[768,16,96]{0,2,1:T(8,128)(2,1)}, u32[]{:S(2)}, u32[]{:S(2)}) async-start(bf16[768,16,96]{0,2,1:T(8,128)(2,1)} %bitcast.25), calls=%async_computation.2 | async-start | bytes 4718592 | tf_op jit(solution)/shard_map/all_to_all | solution.py:84
  97.3 4.3 %copy.49 = bf16[768,1536]{0,1:T(8,128)(2,1)} copy(bf16[768,1536]{1,0:T(8,128)(2,1)} %get-tuple-element.16) | data formatting | bytes 4718592 | tf_op jit(solution)/shard_map/convert_element_type | solution.py:80
  101.5 31.9 %all-to-all-done.2 = bf16[768,16,96]{0,2,1:T(8,128)(2,1)} async-done(((bf16[768,16,96]{0,2,1:T(8,128)(2,1)}), bf16[768,16,96]{0,2,1:T(8,128)(2,1)}, u32[]{:S(2)}, u32[]{:S(2)}) %all-to-all-start.2) | async-done | bytes 2359328 | tf_op jit(solution)/shard_map/all_to_all | solution.py:84
  133.4 4.4 %all-to-all-start.3 = ((bf16[768,16,96]{0,2,1:T(8,128)(2,1)}), bf16[768,16,96]{0,2,1:T(8,128)(2,1)}, u32[]{:S(2)}, u32[]{:S(2)}) async-start(bf16[768,16,96]{0,2,1:T(8,128)(2,1)} %bitcast.23), calls=%async_computation.3 | async-start | bytes 4718592 | tf_op jit(solution)/shard_map/all_to_all | solution.py:85
  137.9 0.7 reshape_reshape.3
  140.4 1.6 copy.57
  142.0 3.3 %copy.58 = bf16[16,12,8,768]{3,2,0,1:T(8,128)(2,1)} copy(bf16[16,12,8,768]{3,2,1,0:T(8,128)(2,1)} %bitcast.10) | data formatting | bytes 4718592 | tf_op jit(solution)/shard_map/all_to_all | solution.py:84
  145.3 26.3 %all-to-all-done.3 = bf16[768,16,96]{0,2,1:T(8,128)(2,1)} async-done(((bf16[768,16,96]{0,2,1:T(8,128)(2,1)}), bf16[768,16,96]{0,2,1:T(8,128)(2,1)}, u32[]{:S(2)}, u32[]{:S(2)}) %all-to-all-start.3) | async-done | bytes 2359328 | tf_op jit(solution)/shard_map/all_to_all | solution.py:85
  171.6 3.3 %copy.59 = bf16[16,12,8,768]{3,2,0,1:T(8,128)(2,1)} copy(bf16[16,12,8,768]{3,2,1,0:T(8,128)(2,1)} %bitcast.12) | data formatting | bytes 4718592 | tf_op jit(solution)/shard_map/all_to_all | solution.py:85
  (26 shorter events, 3.3 us)
Async XLA Ops:
  0.6 13.0 %copy-start = (bf16[64,1536]{1,0:T(8,128)(2,1)S(1)}, bf16[64,1536]{1,0:T(8,128)(2,1)}, u32[]{:S(2)}) copy-start(bf16[64,1536]{1,0:T(8,128)(2,1)} %param.13) | copy-start | bytes 589828
  0.6 17.7 %copy-start.5 = (bf16[768,64]{0,1:T(8,128)(2,1)S(1)}, bf16[768,64]{0,1:T(8,128)(2,1)}, u32[]{:S(2)}) copy-start(bf16[768,64]{0,1:T(8,128)(2,1)} %param.18) | copy-start | bytes 294916
  0.7 17.7 %copy-start.3 = (bf16[64,1536]{1,0:T(8,128)(2,1)S(1)}, bf16[64,1536]{1,0:T(8,128)(2,1)}, u32[]{:S(2)}) copy-start(bf16[64,1536]{1,0:T(8,128)(2,1)} %param.19) | copy-start | bytes 589828
  0.7 17.7 %copy-start.1 = (bf16[768,1536]{1,0:T(8,128)(2,1)S(1)}, bf16[768,1536]{1,0:T(8,128)(2,1)}, u32[]{:S(2)}) copy-start(bf16[768,1536]{1,0:T(8,128)(2,1)} %param.17) | copy-start | bytes 7077892
  2.1 22.3 %all-to-all-start.4 = ((bf16[64,1,96]{2,1,0:T(2,128)(2,1)}), bf16[64,1,96]{2,1,0:T(2,128)(2,1)S(1)}, u32[]{:S(2)}, u32[]{:S(2)}) async-start(bf16[64,1,96]{2,1,0:T(2,128)(2,1)} %broadcast_in_dim.13), calls=%async_computation.4 | async-start | bytes 65536 | tf_op jit(solution)/shard_map/all_to_all | solution.py:18
  18.4 3.0 %copy-start.2 = (bf16[768,1536]{1,0:T(8,128)(2,1)S(1)}, bf16[768,1536]{1,0:T(8,128)(2,1)}, u32[]{:S(2)}) copy-start(bf16[768,1536]{1,0:T(8,128)(2,1)} %param.14) | copy-start | bytes 7077892
  18.4 3.0 %copy-start.4 = (bf16[64,1536]{1,0:T(8,128)(2,1)S(1)}, bf16[64,1536]{1,0:T(8,128)(2,1)}, u32[]{:S(2)}) copy-start(bf16[64,1536]{1,0:T(8,128)(2,1)} %param.16) | copy-start | bytes 589828
  18.4 3.0 %copy-start.6 = (bf16[768,64]{0,1:T(8,128)(2,1)S(1)}, bf16[768,64]{0,1:T(8,128)(2,1)}, u32[]{:S(2)}) copy-start(bf16[768,64]{0,1:T(8,128)(2,1)} %param.15) | copy-start | bytes 294916
  25.3 15.9 %all-to-all-start = ((f32[16,1,4608]{2,1,0:T(1,128)}), f32[16,1,4608]{2,1,0:T(1,128)S(1)}, u32[]{:S(2)}, u32[]{:S(2)}) async-start(f32[16,1,4608]{2,1,0:T(1,128)} %broadcast_in_dim.12), calls=%async_computation | async-start | bytes 589824 | tf_op jit(solution)/shard_map/all_to_all | solution.py:18
  41.8 8.8 %all-to-all-start.5 = ((bf16[2,64,96]{2,1,0:T(8,128)(2,1)}), bf16[2,64,96]{2,1,0:T(8,128)(2,1)S(1)}, u32[]{:S(2)}, u32[]{:S(2)}) async-start(bf16[2,64,96]{2,1,0:T(8,128)(2,1)} %broadcast_in_dim.14), calls=%async_computation.5 | async-start | bytes 65536 | tf_op jit(solution)/shard_map/all_to_all | solution.py:18
  50.6 42.2 %all-to-all-start.1 = ((bf16[768,16,96]{0,2,1:T(8,128)(2,1)}), bf16[768,16,96]{0,2,1:T(8,128)(2,1)S(1)}, u32[]{:S(2)}, u32[]{:S(2)}) async-start(bf16[768,16,96]{0,2,1:T(8,128)(2,1)} %bitcast.24), calls=%async_computation.1 | async-start | bytes 4718592 | tf_op jit(solution)/shard_map/all_to_all | solution.py:83
  92.8 40.6 %all-to-all-start.2 = ((bf16[768,16,96]{0,2,1:T(8,128)(2,1)}), bf16[768,16,96]{0,2,1:T(8,128)(2,1)}, u32[]{:S(2)}, u32[]{:S(2)}) async-start(bf16[768,16,96]{0,2,1:T(8,128)(2,1)} %bitcast.25), calls=%async_computation.2 | async-start | bytes 4718592 | tf_op jit(solution)/shard_map/all_to_all | solution.py:84
  133.4 38.1 %all-to-all-start.3 = ((bf16[768,16,96]{0,2,1:T(8,128)(2,1)}), bf16[768,16,96]{0,2,1:T(8,128)(2,1)}, u32[]{:S(2)}, u32[]{:S(2)}) async-start(bf16[768,16,96]{0,2,1:T(8,128)(2,1)} %bitcast.23), calls=%async_computation.3 | async-start | bytes 4718592 | tf_op jit(solution)/shard_map/all_to_all | solution.py:85
where the time goes:
time: 176 us; the launch traced here: 175 us
  waiting for transfers between devices  94 us (53%)
  starting transfers between devices  34.4 us (20%)
  local copies, waits for them, and re-layouts  23.8 us (14%)
  other arithmetic  11.1 us (6%)
  matrix products  10.7 us (6%)
    all_to_all x1, waiting for transfers between devices, local(): lax.all_to_all(narrow_key, FSDP, split_axis=1, concat_axis=0, tiled=True)  31.9 us
    all_to_all x1, waiting for transfers between devices, local(): lax.all_to_all(narrow_query, FSDP, split_axis=1, concat_axis=0, tiled=True)  27 us
    all_to_all x1, waiting for transfers between devices, local(): lax.all_to_all(narrow_value, FSDP, split_axis=1, concat_axis=0, tiled=True)  26.3 us
    all_to_all x3, starting transfers between devices, copy_for_each(): return lax.all_to_all(copies, axis, split_axis=0, concat_axis=0, tiled=True)  21.8 us
    all_to_all x3, waiting for transfers between devices, copy_for_each(): return lax.all_to_all(copies, axis, split_axis=0, concat_axis=0, tiled=True)  8.86 us
    convert_element_type x1, other arithmetic, local(): (latest_value / factor_value).astype(jnp.bfloat16)  7.21 us
    dot_general x1, matrix products, local(): jnp.dot(low_query, high_query, preferred_element_type=jnp.float32)  4.66 us
    all_to_all x1, starting transfers between devices, local(): lax.all_to_all(narrow_key, FSDP, split_axis=1, concat_axis=0, tiled=True)  4.45 us
  transfers between devices with their start and end apart: 6, of which 4 were waited for; matrix products, arithmetic and copies ran while one was open for 22% of the time, Pallas kernels for 0%

commit v1 on v0

v1 whole, which is shorter than its diff:
```python
import functools

import jax
import jax.numpy as jnp
from jax import lax
from jax.experimental import pallas as pl
from jax.experimental.pallas import tpu as pltpu
from jax.sharding import PartitionSpec as P

MESH = pl.DeviceIdType.MESH
mix_rate = 2.0

Z = X = 4
TP = 8
ROWS = 768
COLS = 1536
MINE = 96
HALF = MINE // 2
GROUP = MINE * X
RANK = 64
WHOLE = 12288
STEPS = (1, 3, 2)
DIAGONAL = [(a, b) for a in STEPS for b in STEPS]


def rows_at(start, size):
    return pl.ds(pl.multiple_of(start, 16), size)


def lanes_at(start, size):
    return pl.ds(pl.multiple_of(start, 128), size)


def kernel(
    w0, l0, h0, w1, l1, h1, w2, l2, h2, train, step,
    o0, o1, o2, f0, f1, f2, norm,
    w, low, high, latest, turned, rel_z, rel_x, max_z, max_x, inverse, adds, gains,
    load_sem, max_send, max_recv, gain_send, gain_recv, send, recv, own_sem,
):
    me = lax.axis_index("fsdp")
    tp = lax.axis_index("tp")
    z, x = me // X, me % X
    outs, factors = (o0, o1, o2), (f0, f1, f2)

    def at(dz, dx):
        return ((z + dz) % Z) * X + (x + dx) % X

    def remote(src, dst, s, r, dz, dx):
        return pltpu.make_async_remote_copy(
            src, dst, s, r, device_id={"fsdp": at(dz, dx)}, device_id_type=MESH
        )

    loads = []
    for m, (a, b, c) in enumerate(((w0, l0, h0), (w1, l1, h1), (w2, l2, h2))):
        loads.append(
            [
                pltpu.make_async_copy(b, low.at[m], load_sem.at[3 * m + 1]),
                pltpu.make_async_copy(c, high.at[m], load_sem.at[3 * m + 2]),
                pltpu.make_async_copy(a, w.at[m], load_sem.at[3 * m]),
            ]
        )
    extra = [
        pltpu.make_async_copy(train, adds.at[0], load_sem.at[9]),
        pltpu.make_async_copy(step, adds.at[1], load_sem.at[10]),
    ]
    for c in (*loads[0], *extra, *loads[1], *loads[2]):
        c.start()

    barrier = pltpu.get_barrier_semaphore()
    for d in (1, 2, 3):
        for peer in (at(d, 0), at(0, d)):
            pl.semaphore_signal(barrier, 1, device_id={"fsdp": peer}, device_id_type=MESH)
    for d in range(1, TP):
        pl.semaphore_signal(
            barrier, 1, device_id={"tp": (tp + d) % TP}, device_id_type=MESH
        )

    eye = (
        lax.broadcasted_iota(jnp.int32, (128, 128), 0)
        == lax.broadcasted_iota(jnp.int32, (128, 128), 1)
    ).astype(jnp.bfloat16)

    def merge(m):
        for c in loads[m]:
            c.wait()

        def columns(i, _):
            cols = lanes_at(i * 256, 256)
            most = jnp.zeros((1, 256), jnp.float32)
            for r in range(0, ROWS, 256):
                product = lax.dot_general(
                    low[m, :, r : r + 256],
                    high[m, :, cols],
                    (((0,), (0,)), ((), ())),
                    preferred_element_type=jnp.float32,
                )
                sums = w[m, r : r + 256, cols].astype(jnp.float32) + mix_rate * product
                latest[m, r : r + 256, cols] = sums
                most = jnp.maximum(most, jnp.max(jnp.abs(sums), axis=0, keepdims=True))
            max_z[m, z, :, cols] = most
            return 0

        lax.fori_loop(0, COLS // 256, columns, 0)

    def max_copies(m, stage):
        buffer, place = ((max_z, z), (max_x, x))[stage]
        return [
            remote(
                buffer.at[m, place],
                buffer.at[m, place],
                max_send.at[m, stage, d - 1],
                max_recv.at[m, stage, d - 1],
                *((d, 0) if stage == 0 else (0, d)),
            )
            for d in STEPS
        ]

    def start(copies):
        for c in copies:
            c.start()
        return copies

    def largest(buffer, m):
        return jnp.maximum(
            jnp.maximum(buffer[m, 0], buffer[m, 1]), jnp.maximum(buffer[m, 2], buffer[m, 3])
        )

    def wait_recv(copies):
        for c in copies:
            c.wait_recv()

    def second_stage(m, first):
        wait_recv(first)
        max_x[m, x] = largest(max_z, m)
        return start(max_copies(m, 1))

    def finish_max(m, second):
        wait_recv(second)
        factor = largest(max_x, m)
        factors[m][...] = pltpu.roll(factor, (COLS - MINE * me) % COLS, 1)[:, :MINE]
        inverse[m] = 1.0 / factor

    def turn(m, dz):
        base = ((z + dz) % Z) * GROUP
        for j in range(0, GROUP, 128):
            cols = lanes_at(base + j, 128)
            ready = (latest[m, :, cols] * inverse[m, :, cols]).astype(jnp.bfloat16)
            turned[m, lanes_at(base + j, 128), :] = lax.dot_general(
                eye, ready, (((1,), (1,)), ((), ())), preferred_element_type=jnp.float32
            ).astype(jnp.bfloat16)

    def block(m, dz, dx, first, size):
        return turned.at[m, rows_at(at(dz, dx) * MINE + first, size), :]

    def place_of(m, first, size, dz, dx):
        return outs[m].at[first : first + size, lanes_at(at(dz, dx) * ROWS, ROWS)]

    def straight(m, dz, dx):
        n = dz - 1 if dz else 2 + dx
        return remote(
            block(m, dz, dx, 0, MINE),
            place_of(m, 0, MINE, 0, 0),
            send.at[m, n],
            recv.at[m, n],
            dz,
            dx,
        )

    def number(dz, dx):
        return 3 * (dz - 1) + dx - 1

    def first_z(m, dz, dx):
        n = 6 + number(dz, dx)
        return remote(
            block(m, dz, dx, 0, HALF),
            rel_z.at[m, dz - 1, dx - 1],
            send.at[m, n],
            recv.at[m, n],
            dz,
            0,
        )

    def first_x(m, dz, dx):
        n = 15 + number(dz, dx)
        return remote(
            block(m, dz, dx, HALF, HALF),
            rel_x.at[m, dz - 1, dx - 1],
            send.at[m, n],
            recv.at[m, n],
            0,
            dx,
        )

    def then_x(m, dz, dx):
        n = 24 + number(dz, dx)
        return remote(
            rel_z.at[m, dz - 1, dx - 1],
            place_of(m, 0, HALF, -dz, 0),
            send.at[m, n],
            recv.at[m, n],
            0,
            dx,
        )

    def then_z(m, dz, dx):
        n = 33 + number(dz, dx)
        return remote(
            rel_x.at[m, dz - 1, dx - 1],
            place_of(m, HALF, HALF, 0, -dx),
            send.at[m, n],
            recv.at[m, n],
            dz,
            0,
        )

    sent, landing = [], []

    def send_group(m):
        relayed = []
        for dz in (*STEPS, 0):
            turn(m, dz)
            if dz:
                direct = [straight(m, dz, 0)]
                hops = [c(m, dz, dx) for dx in STEPS for c in (first_x, first_z)]
            else:
                direct = [straight(m, 0, dx) for dx in STEPS]
                hops = []
            start(direct)
            start(hops)
            sent.extend(direct + hops)
            landing.extend(direct)
            relayed.extend(hops)
        own = pltpu.make_async_copy(
            block(m, 0, 0, 0, MINE), place_of(m, 0, MINE, 0, 0), own_sem.at[m]
        )
        own.start()
        owns.append(own)

    owns = []

    def relay(m):
        for dz, dx in DIAGONAL:
            first_x(m, dz, dx).wait_recv()
            a = then_z(m, dz, dx)
            a.start()
            first_z(m, dz, dx).wait_recv()
            b = then_x(m, dz, dx)
            b.start()
            sent.extend((a, b))
            landing.extend((a, b))

    merge(0)
    pl.semaphore_wait(barrier, 13)
    first = [start(max_copies(0, 0))]

    for c in extra:
        c.wait()
    gains[z, x, tp, :, 0:MINE] = adds[0] + adds[1]

    def gain_copy(part, n, **device):
        return pltpu.make_async_remote_copy(
            part, part, gain_send.at[n], gain_recv.at[n], device_id=device, device_id_type=MESH
        )

    gain_z = start([gain_copy(gains.at[z, x, tp], d - 1, fsdp=at(d, 0)) for d in STEPS])

    merge(1)
    second = [second_stage(0, first[0])]
    first.append(start(max_copies(1, 0)))
    merge(2)
    first.append(start(max_copies(2, 0)))
    finish_max(0, second[0])
    send_group(0)
    second.append(second_stage(1, first[1]))
    second.append(second_stage(2, first[2]))
    wait_recv(gain_z)
    gain_x = start([gain_copy(gains.at[:, x, tp], 2 + d, fsdp=at(0, d)) for d in STEPS])
    finish_max(1, second[1])
    send_group(1)
    finish_max(2, second[2])
    wait_recv(gain_x)
    gain_tp = start(
        [gain_copy(gains.at[:, :, tp], 5 + d, tp=(tp + d) % TP) for d in range(1, TP)]
    )
    relay(0)
    send_group(2)
    relay(1)
    relay(2)
    wait_recv(gain_tp)
    norm[...] = gains[...]
    wait_recv(landing)
    for c in owns:
        c.wait()
    for c in (*sum(first, []), *sum(second, []), *gain_z, *gain_x, *gain_tp, *sent):
        c.wait_send()


def local(w0, l0, h0, w1, l1, h1, w2, l2, h2, train, step):
    f32, bf16 = jnp.float32, jnp.bfloat16
    vmem = pl.BlockSpec(memory_space=pltpu.VMEM)
    dma = pltpu.SemaphoreType.DMA
    o0, o1, o2, f0, f1, f2, norm = pl.pallas_call(
        kernel,
        out_shape=[
            *[pltpu.VMEM((MINE, WHOLE), bf16)] * 3,
            *[pltpu.VMEM((1, MINE), f32)] * 3,
            pltpu.VMEM((Z, X, TP, 1, 128), f32),
        ],
        in_specs=[pl.BlockSpec(memory_space=pltpu.HBM)] * 11,
        out_specs=[vmem] * 7,
        scratch_shapes=[
            pltpu.VMEM((3, ROWS, COLS), bf16),
            pltpu.VMEM((3, RANK, ROWS), bf16),
            pltpu.VMEM((3, RANK, COLS), bf16),
            pltpu.VMEM((3, ROWS, COLS), f32),
            pltpu.VMEM((3, COLS, ROWS), bf16),
            pltpu.VMEM((3, 3, 3, HALF, ROWS), bf16),
            pltpu.VMEM((3, 3, 3, HALF, ROWS), bf16),
            pltpu.VMEM((3, Z, 1, COLS), f32),
            pltpu.VMEM((3, X, 1, COLS), f32),
            pltpu.VMEM((3, 1, COLS), f32),
            pltpu.VMEM((2, 1, MINE), f32),
            pltpu.VMEM((Z, X, TP, 1, 128), f32),
            dma((11,)),
            dma((3, 2, 3)),
            dma((3, 2, 3)),
            dma((13,)),
            dma((13,)),
            dma((3, 42)),
            dma((3, 42)),
            dma((3,)),
        ],
        compiler_params=pltpu.CompilerParams(
            collective_id=0, has_side_effects=True, vmem_limit_bytes=42 * 1024 * 1024
        ),
        name="merge_and_spread",
    )(
        w0, l0.T, h0, w1, l1.T, h1, w2, l2.T, h2,
        train.reshape(1, MINE), step.reshape(1, MINE),
    )
    serve = norm.reshape(Z * X * TP, 128)[:, :MINE].reshape(WHOLE).astype(bf16)
    return (
        o0.T, o1.T, o2.T,
        f0.reshape(MINE), f1.reshape(MINE), f2.reshape(MINE),
        serve,
    )


def solution(mesh):
    return jax.shard_map(
        local,
        mesh=mesh,
        in_specs=(
            *(P("fsdp", "tp"), P("fsdp", None), P(None, "tp")) * 3,
            P(("fsdp", "tp")),
            P(("fsdp", "tp")),
        ),
        out_specs=(*[P(None, ("tp", "fsdp"))] * 3, *[P(("tp", "fsdp"))] * 3, P()),
        check_vma=False,
    )
```

time: 176 us -> 113 us (0.64)
  Pallas kernels: 0 us -> 97.4 us
  waiting for transfers between devices: 94 us -> 0 us
  starting transfers between devices: 34.4 us -> 0 us
  other arithmetic: 11.1 us -> 0.05 us
  matrix products: 10.7 us -> 0 us
  local copies, waits for them, and re-layouts: 23.8 us -> 14.9 us
    pallas_call x0 -> x1, Pallas kernels: none -> 97.4 us  [local(): pl.pallas_call(kernel, out_shape=[*[pltpu.VMEM((MINE, WHOLE), bf16)] * 3,...]
    all_to_all x6 -> x0, waiting for transfers between devices: 94 us -> none  [the longest x1 31.9 us: local(): lax.all_to_all(narrow_key, FSDP, split_axis=1, concat_axis=0, tiled=True)]
    all_to_all x6 -> x0, starting transfers between devices: 34.4 us -> none  [the longest x3 21.8 us: copy_for_each(): return lax.all_to_all(copies, axis, split_axis=0, concat_axis=0, tiled=True)]
    unnamed x15 -> x25, local copies, waits for them, and re-layouts: 0.05 us -> 14.2 us
    convert_element_type x3 -> x0, other arithmetic: 10.9 us -> none  [the longest x1 7.21 us: local(): (latest_value / factor_value).astype(jnp.bfloat16)]
    dot_general x3 -> x0, matrix products: 10.7 us -> none  [the longest x1 4.66 us: local(): jnp.dot(low_query, high_query, preferred_element_type=jnp.float32)]
    convert_element_type x3 -> x1, local copies, waits for them, and re-layouts: 11 us -> 0.72 us  [local(): serve = norm.reshape(Z * X * TP, 128)[:, :MINE].reshape(WHOLE).astype(bf16)]
    all_to_all x3 -> x0, local copies, waits for them, and re-layouts: 8.17 us -> none  [the longest x1 3.28 us: local(): lax.all_to_all(narrow_value, FSDP, split_axis=1, concat_axis=0, tiled=True)]
  transfers between devices with their start and end apart: 6 -> 0, of which waited for: 4 -> 0; matrix products, arithmetic and copies ran while one was open for 22% -> 0% of each run, Pallas kernels for 0% -> 0%
where the time goes in v1:
time: 113 us
  Pallas kernels  97.4 us (86%)
  local copies, waits for them, and re-layouts  14.9 us (13%)
    pallas_call x1, Pallas kernels, local(): pl.pallas_call(kernel, out_shape=[*[pltpu.VMEM((MINE, WHOLE), bf16)] * 3,...  97.4 us
    unnamed x25, local copies, waits for them, and re-layouts  14.2 us

profile of v1, /device:TPU:0, one launch (start us, length us, event | category | flops | bytes accessed | tf_op | source)
XLA Modules:
  0.0 113.0 jit_solution(11879982838673088430)
XLA Ops:
  0.6 0.0 copy-start
  0.6 1.7 %copy-done = bf16[768,1536]{1,0:T(8,128)(2,1)S(1)} copy-done((bf16[768,1536]{1,0:T(8,128)(2,1)S(1)}, bf16[768,1536]{1,0:T(8,128)(2,1)}, u32[]{:S(2)}) %copy-start) | copy-done | bytes 2359320
  2.3 0.0 copy-start.1
  2.3 0.9 copy-done.1
  3.2 0.0 copy-start.2
  3.2 0.9 copy-done.2
  4.2 0.0 copy-start.3
  4.2 0.9 copy-done.3
  5.1 0.0 copy-start.4
  5.1 0.9 copy-done.4
  6.0 0.0 copy-start.5
  6.0 0.9 copy-done.5
  6.9 0.0 copy-start.6
  6.9 0.9 copy-done.6
  7.8 0.7 copy-done.7
  8.4 0.7 copy-done.8
  9.1 97.4 %merge_and_spread.1 = (bf16[96,12288]{1,0:T(8,128)(2,1)S(1)}, bf16[96,12288]{1,0:T(8,128)(2,1)S(1)}, bf16[96,12288]{1,0:T(8,128)(2,1)S(1)}, f32[1,96]{1,0:T(1,12...) custom-call(bf16[768,1536]{1,0:T(8,128)(2,1)S(1)} %copy-done, ...), custom_call_target="tpu_custom_call" | custom-call | tf_op jit(solution)/shard_map/merge_and_spread/pallas_call | solution.py:302
  106.4 1.4 %copy.25 = bf16[12288,96]{0,1:T(8,128)(2,1)} copy(bf16[12288,96]{0,1:T(8,128)(2,1)S(1)} %bitcast.15) | data formatting | bytes 4718592
  107.8 1.4 %copy.26 = bf16[12288,96]{0,1:T(8,128)(2,1)} copy(bf16[12288,96]{0,1:T(8,128)(2,1)S(1)} %bitcast.14) | data formatting | bytes 4718592
  109.3 0.5 copy.28
  109.8 0.5 copy.29
  110.3 0.5 copy.30
  110.9 0.7 convert_element_type.4
  111.6 1.4 %copy.27 = bf16[12288,96]{0,1:T(8,128)(2,1)} copy(bf16[12288,96]{0,1:T(8,128)(2,1)S(1)} %bitcast.13) | data formatting | bytes 4718592
  (4 shorter events, 0.1 us)
Async XLA Ops:
  0.6 1.7 %copy-start = (bf16[768,1536]{1,0:T(8,128)(2,1)S(1)}, bf16[768,1536]{1,0:T(8,128)(2,1)}, u32[]{:S(2)}) copy-start(bf16[768,1536]{1,0:T(8,128)(2,1)} %w0.1) | copy-start | bytes 7077892
  2.3 0.9 copy-start.1
  3.2 0.9 copy-start.2
  4.2 0.9 copy-start.3
  5.1 0.9 copy-start.4
  6.0 0.9 copy-start.5
  6.9 0.9 copy-start.6
  7.8 0.7 copy-start.7
  8.4 0.7 copy-start.8

commit v2 on v1

v2 whole, which is shorter than its diff:
```python
import functools

import jax
import jax.numpy as jnp
from jax import lax
from jax.experimental import pallas as pl
from jax.experimental.pallas import tpu as pltpu
from jax.sharding import PartitionSpec as P

MESH = pl.DeviceIdType.MESH
mix_rate = 2.0

Z = X = 4
TP = 8
ROWS = 768
COLS = 1536
MINE = 96
HALF = MINE // 2
GROUP = MINE * X
RANK = 64
WHOLE = 12288
PIECE = ROWS // 2
VMEM = 59_800_000
STEPS = (1, 3, 2)
ROUNDS = [(STEPS[i], STEPS[(i + r) % 3]) for r in range(3) for i in range(3)]


def rows_at(start, size):
    return pl.ds(pl.multiple_of(start, 16), size)


def lanes_at(start, size):
    return pl.ds(pl.multiple_of(start, 128), size)


def kernel(
    w0, l0, h0, w1, l1, h1, w2, l2, h2, train, step,
    o0, o1, o2, f0, f1, f2, norm,
    w, low, high, latest, sums0, turned, rel_z, rel_x, max_z, max_x, inverse, adds, gains, dense, lows,
    load_sem, max_send, max_recv, gain_send, gain_recv, low_send, low_recv, send, recv, own_sem, entered,
):
    me = lax.axis_index("fsdp")
    tp = lax.axis_index("tp")
    z, x = me // X, me % X
    outs, factors = (o0, o1, o2), (f0, f1, f2)

    def at(dz, dx):
        return ((z + dz) % Z) * X + (x + dx) % X

    def remote(src, dst, s, r, dz, dx):
        return pltpu.make_async_remote_copy(
            src, dst, s, r, device_id={"fsdp": at(dz, dx)}, device_id_type=MESH
        )

    y, core = tp // 2, tp % 2
    own_low = lows.at[core, rows_at(16 * y, 16), lanes_at((X * x + z) * PIECE, PIECE)]
    first_loads = [
        pltpu.make_async_copy(
            w0.at[:, j * GROUP : (j + 1) * GROUP],
            w.at[0, :, j * GROUP : (j + 1) * GROUP],
            load_sem.at[j],
        )
        for j in range(Z)
    ]
    loads = [
        [
            pltpu.make_async_copy(a, low.at[m], load_sem.at[4 + 3 * m]),
            pltpu.make_async_copy(b, high.at[m], load_sem.at[5 + 3 * m]),
            pltpu.make_async_copy(c, w.at[1 + m], load_sem.at[6 + 3 * m]),
        ]
        for m, (a, b, c) in enumerate(((l1, h1, w1), (l2, h2, w2)))
    ]
    extra = [
        pltpu.make_async_copy(train, adds.at[0], load_sem.at[10]),
        pltpu.make_async_copy(step, adds.at[1], load_sem.at[11]),
        pltpu.make_async_copy(
            l0.at[rows_at(16 * y, 16), lanes_at(core * PIECE, PIECE)], own_low, load_sem.at[12]
        ),
        pltpu.make_async_copy(h0, high.at[2], load_sem.at[13]),
    ]
    for c in (*first_loads, *loads[0], *loads[1], *extra):
        c.start()

    barrier = pltpu.get_barrier_semaphore()
    for d in (1, 2, 3):
        for peer in (at(d, 0), at(0, d)):
            pl.semaphore_signal(barrier, 1, device_id={"fsdp": peer}, device_id_type=MESH)
    for d in range(1, TP):

        @pl.when(tp + d < TP)
        def _():
            pl.semaphore_signal(
                barrier, 1, device_id={"tp": (tp + d) % TP}, device_id_type=MESH
            )

    eye = (
        lax.broadcasted_iota(jnp.int32, (128, 128), 0)
        == lax.broadcasted_iota(jnp.int32, (128, 128), 1)
    ).astype(jnp.bfloat16)

    def merge(m):
        for c in loads[m]:
            c.wait()

        def columns(i, _):
            cols = lanes_at(i * 256, 256)
            most = jnp.zeros((1, 256), jnp.float32)
            for r in range(0, ROWS, 256):
                product = lax.dot_general(
                    low[m, :, r : r + 256],
                    high[m, :, cols],
                    (((0,), (0,)), ((), ())),
                    preferred_element_type=jnp.float32,
                )
                sums = w[1 + m, r : r + 256, cols].astype(jnp.float32) + mix_rate * product
                latest[m, r : r + 256, cols] = sums
                most = jnp.maximum(most, jnp.max(jnp.abs(sums), axis=0, keepdims=True))
            max_z[z, m, :, cols] = most
            return 0

        lax.fori_loop(0, COLS // 256, columns, 0)

    def max_copies(stage):
        buffer, place = ((max_z, z), (max_x, x))[stage]
        return [
            remote(
                buffer.at[place],
                buffer.at[place],
                max_send.at[stage, d - 1],
                max_recv.at[stage, d - 1],
                *((d, 0) if stage == 0 else (0, d)),
            )
            for d in STEPS
        ]

    def start(copies):
        for c in copies:
            c.start()
        return copies

    def largest(buffer):
        return jnp.maximum(
            jnp.maximum(buffer[0], buffer[1]), jnp.maximum(buffer[2], buffer[3])
        )

    def wait_recv(copies):
        for c in copies:
            c.wait_recv()

    def transposed(block):
        return lax.dot_general(
            eye, block, (((1,), (1,)), ((), ())), preferred_element_type=jnp.float32
        ).astype(jnp.bfloat16)

    def turn(m):
        def columns(i, _):
            cols = lanes_at(i * 128, 128)
            ready = latest[m, :, cols] * inverse[m, :, cols]
            turned[1 + m, cols, :] = transposed(ready.astype(jnp.bfloat16))
            return 0

        lax.fori_loop(0, COLS // 128, columns, 0)

    def turn_first():
        for j, c in enumerate(first_loads):
            c.wait()
            for i in range(j * GROUP, (j + 1) * GROUP, 128):
                turned[0, i : i + 128, :] = transposed(w[0, :, i : i + 128])

    def finish_first():
        mine = pltpu.roll(high[2].astype(jnp.float32), (COLS - MINE * me) % COLS, 1)
        mine = mine[:, :MINE].astype(jnp.bfloat16)

        def place(i):
            p, c = i // 2, i % 2
            at_source = ((p % Z) * X + p // Z) * ROWS + c * PIECE
            return c, lanes_at(p * PIECE, PIECE), lanes_at(at_source, PIECE)

        def add(i, most):
            c, there, here = place(i)
            product = lax.dot_general(
                mine,
                lows[c, :, there],
                (((0,), (0,)), ((), ())),
                preferred_element_type=jnp.float32,
            )
            sums = o0[:, here].astype(jnp.float32) + mix_rate * product
            sums0[:, here] = sums
            sums = jnp.abs(sums)
            for j in range(0, PIECE, 128):
                most = jnp.maximum(most, sums[:, j : j + 128])
            return most

        most = lax.fori_loop(0, 2 * Z * X, add, jnp.zeros((MINE, 128), jnp.float32))
        factor = jnp.max(most, axis=1, keepdims=True)
        same = lax.broadcasted_iota(jnp.int32, (MINE, MINE), 0) == lax.broadcasted_iota(
            jnp.int32, (MINE, MINE), 1
        )
        f0[...] = jnp.max(jnp.where(same, factor, 0.0), axis=0, keepdims=True)
        scale = 1.0 / factor

        def divide(i, _):
            here = lanes_at(i * PIECE, PIECE)
            o0[:, here] = (sums0[:, here] * scale).astype(jnp.bfloat16)
            return 0

        lax.fori_loop(0, 2 * Z * X, divide, 0)

    def block(m, dz, dx, first, size):
        return turned.at[m, rows_at(at(dz, dx) * MINE + first, size), :]

    def place_of(m, first, size, dz, dx):
        return outs[m].at[first : first + size, lanes_at(at(dz, dx) * ROWS, ROWS)]

    def straight(m, dz, dx):
        n = dz - 1 if dz else 2 + dx
        return remote(
            block(m, dz, dx, 0, MINE),
            place_of(m, 0, MINE, 0, 0),
            send.at[m, n],
            recv.at[m, n],
            dz,
            dx,
        )

    def number(dz, dx):
        return 3 * (dz - 1) + dx - 1

    def first_z(m, dz, dx):
        n = 6 + number(dz, dx)
        return remote(
            block(m, dz, dx, 0, HALF),
            rel_z.at[m, dz - 1, dx - 1],
            send.at[m, n],
            recv.at[m, n],
            dz,
            0,
        )

    def first_x(m, dz, dx):
        n = 15 + number(dz, dx)
        return remote(
            block(m, dz, dx, HALF, HALF),
            rel_x.at[m, dz - 1, dx - 1],
            send.at[m, n],
            recv.at[m, n],
            0,
            dx,
        )

    def then_x(m, dz, dx):
        n = 24 + number(dz, dx)
        return remote(
            rel_z.at[m, dz - 1, dx - 1],
            place_of(m, 0, HALF, -dz, 0),
            send.at[m, n],
            recv.at[m, n],
            0,
            dx,
        )

    def then_z(m, dz, dx):
        n = 33 + number(dz, dx)
        return remote(
            rel_x.at[m, dz - 1, dx - 1],
            place_of(m, HALF, HALF, 0, -dx),
            send.at[m, n],
            recv.at[m, n],
            dz,
            0,
        )

    sent, landing, owns = [], [[], [], []], []

    def send_hops(m):
        sent.extend(
            start(
                [c(m, *d) for a, b in ROUNDS for c, d in ((first_z, (a, b)), (first_x, (b, a)))]
            )
        )

    def send_straight(m):
        copies = start([straight(m, *d) for a in STEPS for d in ((a, 0), (0, a))])
        sent.extend(copies)
        landing[m].extend(copies)
        own = pltpu.make_async_copy(
            block(m, 0, 0, 0, MINE), place_of(m, 0, MINE, 0, 0), own_sem.at[m]
        )
        own.start()
        owns.append(own)

    def relay(m):
        for a, b in ROUNDS:
            first_x(m, a, b).wait_recv()
            first_z(m, b, a).wait_recv()
            sent.extend(start([then_z(m, a, b), then_x(m, b, a)]))
            landing[m].extend(sent[-2:])

    turn_first()
    pl.semaphore_wait(barrier, 6 + tp)
    send_hops(0)
    for d in range(1, TP):

        @pl.when(d <= tp)
        def _():
            pl.semaphore_signal(
                entered, 1, device_id={"tp": (tp + TP - d) % TP}, device_id_type=MESH
            )

    def share(part, s, r, n, **device):
        return pltpu.make_async_remote_copy(
            part, part, s.at[n], r.at[n], device_id=device, device_id_type=MESH
        )

    def gather(stage):
        if stage == 0:
            parts = gains.at[z, x, tp], own_low
            targets = [(d - 1, {"fsdp": at(d, 0)}) for d in STEPS]
        elif stage == 1:
            lanes = lanes_at(X * x * PIECE, Z * PIECE)
            parts = gains.at[:, x, tp], lows.at[core, rows_at(16 * y, 16), lanes]
            targets = [(2 + d, {"fsdp": at(0, d)}) for d in STEPS]
        else:
            parts = gains.at[:, :, tp], lows.at[core, rows_at(16 * y, 16), :]
            targets = [(5 + d, {"tp": (tp + d) % TP}) for d in range(1, TP)]
        sems = (gain_send, gain_recv), (low_send, low_recv)
        return start([share(p, *q, n, **t) for n, t in targets for p, q in zip(parts, sems)])

    merge(0)
    merge(1)
    small = [start(max_copies(0))]
    for c in extra:
        c.wait()
    gains[z, x, tp, :, 0:MINE] = adds[0] + adds[1]
    small.append(gather(0))
    send_straight(0)
    wait_recv(small[0])
    max_x[x] = largest(max_z)
    small.append(start(max_copies(1)))
    wait_recv(small[1])
    small.append(gather(1))
    relay(0)
    wait_recv(small[2])
    factor = largest(max_x)
    inverse[...] = 1.0 / factor
    for m in (0, 1):
        outputs = pltpu.roll(factor[m], (COLS - MINE * me) % COLS, 1)
        factors[1 + m][...] = outputs[:, :MINE]
    turn(0)
    send_hops(1)
    send_straight(1)
    wait_recv(small[3])

    @pl.when(tp < TP - 1)
    def _():
        pl.semaphore_wait(entered, TP - 1 - tp)

    small.append(gather(2))
    turn(1)
    send_hops(2)
    send_straight(2)
    wait_recv(landing[0])
    owns[0].wait()
    wait_recv(small[4])
    finish_first()
    relay(1)
    relay(2)
    lane = lax.broadcasted_iota(jnp.int32, (1, 128), 1)

    def pack(g, _):
        f, t = g // 2, 4 * (g % 2)
        a, b, c, d = (gains[f // X, f % X, t + j] for j in range(4))
        b, c, d = pltpu.roll(b, 96, 1), pltpu.roll(c, 64, 1), pltpu.roll(d, 32, 1)
        dense[pl.ds(3 * g, 1), :] = jnp.where(lane < 96, a, b)
        dense[pl.ds(3 * g + 1, 1), :] = jnp.where(lane < 64, b, c)
        dense[pl.ds(3 * g + 2, 1), :] = jnp.where(lane < 32, c, d)
        return 0

    lax.fori_loop(0, Z * X * TP // 4, pack, 0)
    norm[...] = dense[...].astype(jnp.bfloat16)
    wait_recv(landing[1] + landing[2])
    for c in owns[1:]:
        c.wait()
    for c in (*sum(small, []), *sent):
        c.wait_send()


def write_out(*refs):
    copies = [
        pltpu.make_async_copy(a, b, refs[14].at[n])
        for n, (a, b) in enumerate(zip(refs[:7], refs[7:14]))
    ]
    for c in copies:
        c.start()
    for c in copies:
        c.wait()


def local(w0, l0, h0, w1, l1, h1, w2, l2, h2, train, step):
    f32, bf16 = jnp.float32, jnp.bfloat16
    vmem = pl.BlockSpec(memory_space=pltpu.VMEM)
    dma = pltpu.SemaphoreType.DMA
    gathered = pl.pallas_call(
        kernel,
        out_shape=[
            *[pltpu.VMEM((MINE, WHOLE), bf16)] * 3,
            *[pltpu.VMEM((1, MINE), f32)] * 3,
            pltpu.VMEM((WHOLE // 128, 128), bf16),
        ],
        in_specs=[pl.BlockSpec(memory_space=pltpu.HBM)] * 11,
        out_specs=[vmem] * 7,
        scratch_shapes=[
            pltpu.VMEM((3, ROWS, COLS), bf16),
            pltpu.VMEM((2, RANK, ROWS), bf16),
            pltpu.VMEM((3, RANK, COLS), bf16),
            pltpu.VMEM((2, ROWS, COLS), f32),
            pltpu.VMEM((MINE, WHOLE), f32),
            pltpu.VMEM((3, COLS, ROWS), bf16),
            pltpu.VMEM((3, 3, 3, HALF, ROWS), bf16),
            pltpu.VMEM((3, 3, 3, HALF, ROWS), bf16),
            pltpu.VMEM((Z, 2, 1, COLS), f32),
            pltpu.VMEM((X, 2, 1, COLS), f32),
            pltpu.VMEM((2, 1, COLS), f32),
            pltpu.VMEM((2, 1, MINE), f32),
            pltpu.VMEM((Z, X, TP, 1, 128), f32),
            pltpu.VMEM((MINE, 128), f32),
            pltpu.VMEM((2, RANK, Z * X * PIECE), bf16),
            dma((14,)),
            dma((2, 3)),
            dma((2, 3)),
            dma((13,)),
            dma((13,)),
            dma((13,)),
            dma((13,)),
            dma((3, 42)),
            dma((3, 42)),
            dma((3,)),
            pltpu.SemaphoreType.REGULAR,
        ],
        compiler_params=pltpu.CompilerParams(
            collective_id=0, has_side_effects=True, vmem_limit_bytes=VMEM
        ),
        name="merge_and_spread",
    )(
        w0, l0.T, h0, w1, l1.T, h1, w2, l2.T, h2,
        train.reshape(1, MINE), step.reshape(1, MINE),
    )
    o0, o1, o2, f0, f1, f2, norm = pl.pallas_call(
        write_out,
        out_shape=[jax.ShapeDtypeStruct(a.shape, a.dtype) for a in gathered],
        in_specs=[pl.BlockSpec(memory_space=pl.ANY)] * 7,
        out_specs=[pl.BlockSpec(memory_space=pltpu.HBM)] * 7,
        scratch_shapes=[dma((7,))],
        compiler_params=pltpu.CompilerParams(vmem_limit_bytes=1024 * 1024),
        name="write_out",
    )(*gathered)
    return (
        o0.T, o1.T, o2.T,
        f0.reshape(MINE), f1.reshape(MINE), f2.reshape(MINE),
        norm.reshape(WHOLE),
    )


def solution(mesh):
    return jax.shard_map(
        local,
        mesh=mesh,
        in_specs=(
            *(P("fsdp", "tp"), P("fsdp", None), P(None, "tp")) * 3,
            P(("fsdp", "tp")),
            P(("fsdp", "tp")),
        ),
        out_specs=(*[P(None, ("tp", "fsdp"))] * 3, *[P(("tp", "fsdp"))] * 3, P()),
        check_vma=False,
    )
```

time: 113 us -> 93.3 us (0.83)
  local copies, waits for them, and re-layouts: 14.9 us -> 0 us
  Pallas kernels: 97.4 us -> 92.5 us
    unnamed x25 -> x0, local copies, waits for them, and re-layouts: 14.2 us -> none
    pallas_call x1, Pallas kernels: 97.4 us -> 89.5 us  [local(): pl.pallas_call(kernel, out_shape=[*[pltpu.VMEM((MINE, WHOLE), bf16)] * 3,...]
    pallas_call x0 -> x1, Pallas kernels: none -> 3.03 us  [local(): pl.pallas_call(write_out, out_shape=[jax.ShapeDtypeStruct(a.shape, a.dtyp...]
where the time goes in v2:
time: 93.3 us; the launch traced here: 93.2 us
  Pallas kernels  92.5 us (99%)
    pallas_call x1, Pallas kernels, local(): pl.pallas_call(kernel, out_shape=[*[pltpu.VMEM((MINE, WHOLE), bf16)] * 3,...  89.5 us
    pallas_call x1, Pallas kernels, local(): pl.pallas_call(write_out, out_shape=[jax.ShapeDtypeStruct(a.shape, a.dtyp...  3.03 us

profile of v2, /device:TPU:0, one launch (start us, length us, event | category | flops | bytes accessed | tf_op | source)
XLA Modules:
  0.0 93.2 jit_solution(1255199970641986064)
XLA Ops:
  0.6 89.5 %merge_and_spread.1 = (bf16[96,12288]{1,0:T(8,128)(2,1)S(1)}, bf16[96,12288]{1,0:T(8,128)(2,1)S(1)}, bf16[96,12288]{1,0:T(8,128)(2,1)S(1)}, f32[1,96]{1,0:T(1,12...) custom-call(bf16[768,1536]{1,0:T(8,128)(2,1)} %w0.1, bf16[64,768]{1,0:T(8,128)(2,1)} %bitcast.12, ...), custom_call_target="tpu_custom_call" | custom-call | tf_op jit(solution)/shard_map/merge_and_spread/pallas_call | solution.py:403
  90.2 3.0 %write_out.1 = (bf16[96,12288]{1,0:T(8,128)(2,1)}, bf16[96,12288]{1,0:T(8,128)(2,1)}, bf16[96,12288]{1,0:T(8,128)(2,1)}, f32[1,96]{1,0:T(1,128)}, f32[1,96]{1,0:...) custom-call(bf16[96,12288]{1,0:T(8,128)(2,1)S(1)} %get-tuple-element.21.refs_0_, ...), custom_call_target="tpu_custom_call" | custom-call | tf_op jit(solution)/shard_map/write_out/pallas_call | solution.py:448

commit v3 on v2

--- a/solution.py
+++ b/solution.py
@@ -23,6 +23,7 @@
 VMEM = 59_800_000
 STEPS = (1, 3, 2)
 ROUNDS = [(STEPS[i], STEPS[(i + r) % 3]) for r in range(3) for i in range(3)]
+LAST = sorted(ROUNDS, key=lambda d: d[0] != 2)
 
 
 def rows_at(start, size):
@@ -53,7 +54,8 @@
         )
 
     y, core = tp // 2, tp % 2
-    own_low = lows.at[core, rows_at(16 * y, 16), lanes_at((X * x + z) * PIECE, PIECE)]
+    major, minor = x + core * (z - x), z + core * (x - z)
+    own_low = lows.at[core, rows_at(16 * y, 16), lanes_at((X * major + minor) * PIECE, PIECE)]
     first_loads = [
         pltpu.make_async_copy(
             w0.at[:, j * GROUP : (j + 1) * GROUP],
@@ -78,9 +80,6 @@
         ),
         pltpu.make_async_copy(h0, high.at[2], load_sem.at[13]),
     ]
-    for c in (*first_loads, *loads[0], *loads[1], *extra):
-        c.start()
-
     barrier = pltpu.get_barrier_semaphore()
     for d in (1, 2, 3):
         for peer in (at(d, 0), at(0, d)):
@@ -92,6 +91,9 @@
             pl.semaphore_signal(
                 barrier, 1, device_id={"tp": (tp + d) % TP}, device_id_type=MESH
             )
+
+    for c in (*first_loads, *loads[0], *loads[1], *extra):
+        c.start()
 
     eye = (
         lax.broadcasted_iota(jnp.int32, (128, 128), 0)
@@ -173,7 +175,8 @@
 
         def place(i):
             p, c = i // 2, i % 2
-            at_source = ((p % Z) * X + p // Z) * ROWS + c * PIECE
+            a, b = p // X, p % X
+            at_source = ((b + c * (a - b)) * X + a + c * (b - a)) * ROWS + c * PIECE
             return c, lanes_at(p * PIECE, PIECE), lanes_at(at_source, PIECE)
 
         def add(i, most):
@@ -272,12 +275,11 @@
 
     sent, landing, owns = [], [[], [], []], []
 
+    def hops_of(m):
+        return [c(m, *d) for a, b in ROUNDS for c, d in ((first_z, (a, b)), (first_x, (b, a)))]
+
     def send_hops(m):
-        sent.extend(
-            start(
-                [c(m, *d) for a, b in ROUNDS for c, d in ((first_z, (a, b)), (first_x, (b, a)))]
-            )
-        )
+        sent.extend(start(hops_of(m)))
 
     def send_straight(m):
         copies = start([straight(m, *d) for a in STEPS for d in ((a, 0), (0, a))])
@@ -290,7 +292,7 @@
         owns.append(own)
 
     def relay(m):
-        for a, b in ROUNDS:
+        for a, b in (ROUNDS if m < 2 else LAST):
             first_x(m, a, b).wait_recv()
             first_z(m, b, a).wait_recv()
             sent.extend(start([then_z(m, a, b), then_x(m, b, a)]))
@@ -298,7 +300,13 @@
 
     turn_first()
     pl.semaphore_wait(barrier, 6 + tp)
-    send_hops(0)
+    at_first = hops_of(0)
+    sent.extend(at_first)
+
+    @pl.when(core == 1)
+    def _():
+        start(at_first)
+
     for d in range(1, TP):
 
         @pl.when(d <= tp)
@@ -314,24 +322,29 @@
 
     def gather(stage):
         if stage == 0:
-            parts = gains.at[z, x, tp], own_low
-            targets = [(d - 1, {"fsdp": at(d, 0)}) for d in STEPS]
+            parts = gains.at[core, major, minor, y], own_low
+            targets = [(d - 1, {"fsdp": at(d - core * d, core * d)}) for d in STEPS]
         elif stage == 1:
-            lanes = lanes_at(X * x * PIECE, Z * PIECE)
-            parts = gains.at[:, x, tp], lows.at[core, rows_at(16 * y, 16), lanes]
-            targets = [(2 + d, {"fsdp": at(0, d)}) for d in STEPS]
+            lanes = lanes_at(X * major * PIECE, X * PIECE)
+            parts = gains.at[core, major, :, y], lows.at[core, rows_at(16 * y, 16), lanes]
+            targets = [(2 + d, {"fsdp": at(core * d, d - core * d)}) for d in STEPS]
         else:
-            parts = gains.at[:, :, tp], lows.at[core, rows_at(16 * y, 16), :]
+            parts = gains.at[core, :, :, y], lows.at[core, rows_at(16 * y, 16), :]
             targets = [(5 + d, {"tp": (tp + d) % TP}) for d in range(1, TP)]
         sems = (gain_send, gain_recv), (low_send, low_recv)
         return start([share(p, *q, n, **t) for n, t in targets for p, q in zip(parts, sems)])
 
     merge(0)
+
+    @pl.when(core == 0)
+    def _():
+        start(at_first)
+
     merge(1)
     small = [start(max_copies(0))]
     for c in extra:
         c.wait()
-    gains[z, x, tp, :, 0:MINE] = adds[0] + adds[1]
+    gains[core, major, minor, y, :, 0:MINE] = adds[0] + adds[1]
     small.append(gather(0))
     send_straight(0)
     wait_recv(small[0])
@@ -368,8 +381,10 @@
     lane = lax.broadcasted_iota(jnp.int32, (1, 128), 1)
 
     def pack(g, _):
-        f, t = g // 2, 4 * (g % 2)
-        a, b, c, d = (gains[f // X, f % X, t + j] for j in range(4))
+        f = g // 2
+        p, q, t = f // X, f % X, 2 * (g % 2)
+        a, c = gains[0, q, p, t], gains[0, q, p, t + 1]
+        b, d = gains[1, p, q, t], gains[1, p, q, t + 1]
         b, c, d = pltpu.roll(b, 96, 1), pltpu.roll(c, 64, 1), pltpu.roll(d, 32, 1)
         dense[pl.ds(3 * g, 1), :] = jnp.where(lane < 96, a, b)
         dense[pl.ds(3 * g + 1, 1), :] = jnp.where(lane < 64, b, c)
@@ -378,10 +393,13 @@
 
     lax.fori_loop(0, Z * X * TP // 4, pack, 0)
     norm[...] = dense[...].astype(jnp.bfloat16)
-    wait_recv(landing[1] + landing[2])
     for c in owns[1:]:
         c.wait()
-    for c in (*sum(small, []), *sent):
+    last = len(sent) - 2 * len(LAST)
+    for c in (*sum(small, []), *sent[:last]):
+        c.wait_send()
+    wait_recv(landing[1] + landing[2])
+    for c in sent[last:]:
         c.wait_send()
 
 
@@ -422,7 +440,7 @@
             pltpu.VMEM((X, 2, 1, COLS), f32),
             pltpu.VMEM((2, 1, COLS), f32),
             pltpu.VMEM((2, 1, MINE), f32),
-            pltpu.VMEM((Z, X, TP, 1, 128), f32),
+            pltpu.VMEM((2, X, X, 4, 1, 128), f32),
             pltpu.VMEM((MINE, 128), f32),
             pltpu.VMEM((2, RANK, Z * X * PIECE), bf16),
             dma((14,)),

time: 93.3 us -> 92.3 us (0.989)
  Pallas kernels: 92.5 us -> 91.5 us
    pallas_call x1, Pallas kernels: 89.5 us -> 88.5 us  [local(): pl.pallas_call(kernel, out_shape=[*[pltpu.VMEM((MINE, WHOLE), bf16)] * 3,...]
where the time goes in v3:
time: 92.3 us; the launch traced here: 92.2 us
  Pallas kernels  91.5 us (99%)
    pallas_call x1, Pallas kernels, local(): pl.pallas_call(kernel, out_shape=[*[pltpu.VMEM((MINE, WHOLE), bf16)] * 3,...  88.5 us
    pallas_call x1, Pallas kernels, local(): pl.pallas_call(write_out, out_shape=[jax.ShapeDtypeStruct(a.shape, a.dtyp...  3.03 us

profile of v3, /device:TPU:0, one launch (start us, length us, event | category | flops | bytes accessed | tf_op | source)
XLA Modules:
  0.0 92.2 jit_solution(16840442301936451173)
XLA Ops:
  0.6 88.5 %merge_and_spread.1 = (bf16[96,12288]{1,0:T(8,128)(2,1)S(1)}, bf16[96,12288]{1,0:T(8,128)(2,1)S(1)}, bf16[96,12288]{1,0:T(8,128)(2,1)S(1)}, f32[1,96]{1,0:T(1,12...) custom-call(bf16[768,1536]{1,0:T(8,128)(2,1)} %w0.1, bf16[64,768]{1,0:T(8,128)(2,1)} %bitcast.12, ...), custom_call_target="tpu_custom_call" | custom-call | tf_op jit(solution)/shard_map/merge_and_spread/pallas_call | solution.py:421
  89.1 3.0 %write_out.1 = (bf16[96,12288]{1,0:T(8,128)(2,1)}, bf16[96,12288]{1,0:T(8,128)(2,1)}, bf16[96,12288]{1,0:T(8,128)(2,1)}, f32[1,96]{1,0:T(1,128)}, f32[1,96]{1,0:...) custom-call(bf16[96,12288]{1,0:T(8,128)(2,1)S(1)} %get-tuple-element.21.refs_0_, ...), custom_call_target="tpu_custom_call" | custom-call | tf_op jit(solution)/shard_map/write_out/pallas_call | solution.py:466

commit v4 on v3

--- a/solution.py
+++ b/solution.py
@@ -43,17 +43,18 @@
     me = lax.axis_index("fsdp")
     tp = lax.axis_index("tp")
     z, x = me // X, me % X
+    y, core = tp // 2, tp % 2
+    way = 2 * core - 1
     outs, factors = (o0, o1, o2), (f0, f1, f2)
 
     def at(dz, dx):
-        return ((z + dz) % Z) * X + (x + dx) % X
+        return ((z + way * dz + Z) % Z) * X + (x + way * dx + X) % X
 
     def remote(src, dst, s, r, dz, dx):
         return pltpu.make_async_remote_copy(
             src, dst, s, r, device_id={"fsdp": at(dz, dx)}, device_id_type=MESH
         )
 
-    y, core = tp // 2, tp % 2
     major, minor = x + core * (z - x), z + core * (x - z)
     own_low = lows.at[core, rows_at(16 * y, 16), lanes_at((X * major + minor) * PIECE, PIECE)]
     first_loads = [
@@ -335,13 +336,13 @@
         return start([share(p, *q, n, **t) for n, t in targets for p, q in zip(parts, sems)])
 
     merge(0)
+    merge(1)
+    small = [start(max_copies(0))]
 
     @pl.when(core == 0)
     def _():
         start(at_first)
 
-    merge(1)
-    small = [start(max_copies(0))]
     for c in extra:
         c.wait()
     gains[core, major, minor, y, :, 0:MINE] = adds[0] + adds[1]

time: 92.3 us -> 92.3 us (level)
  no operation moved by 1% of the time
where the time goes in v4:
time: 92.3 us; the launch traced here: 92.2 us
  Pallas kernels  91.5 us (99%)
    pallas_call x1, Pallas kernels, local(): pl.pallas_call(kernel, out_shape=[*[pltpu.VMEM((MINE, WHOLE), bf16)] * 3,...  88.5 us
    pallas_call x1, Pallas kernels, local(): pl.pallas_call(write_out, out_shape=[jax.ShapeDtypeStruct(a.shape, a.dtyp...  3.03 us

profile of v4, /device:TPU:0, one launch (start us, length us, event | category | flops | bytes accessed | tf_op | source)
XLA Modules:
  0.0 92.2 jit_solution(2265026672164971081)
XLA Ops:
  0.6 88.5 %merge_and_spread.1 = (bf16[96,12288]{1,0:T(8,128)(2,1)S(1)}, bf16[96,12288]{1,0:T(8,128)(2,1)S(1)}, bf16[96,12288]{1,0:T(8,128)(2,1)S(1)}, f32[1,96]{1,0:T(1,12...) custom-call(bf16[768,1536]{1,0:T(8,128)(2,1)} %w0.1, bf16[64,768]{1,0:T(8,128)(2,1)} %bitcast.12, ...), custom_call_target="tpu_custom_call" | custom-call | tf_op jit(solution)/shard_map/merge_and_spread/pallas_call | solution.py:422
  89.1 3.0 %write_out.1 = (bf16[96,12288]{1,0:T(8,128)(2,1)}, bf16[96,12288]{1,0:T(8,128)(2,1)}, bf16[96,12288]{1,0:T(8,128)(2,1)}, f32[1,96]{1,0:T(1,128)}, f32[1,96]{1,0:...) custom-call(bf16[96,12288]{1,0:T(8,128)(2,1)S(1)} %get-tuple-element.21.refs_0_, ...), custom_call_target="tpu_custom_call" | custom-call | tf_op jit(solution)/shard_map/write_out/pallas_call | solution.py:467
